TPU v7x, 32 devices: a whole 2x2x4 slice. The times are simulated.
32 devices in a mesh: dp: 2 (over x), tp: 4 (over z), cp: 4 (over y, core).
Axes of the slice: x: 2, y: 2, z: 4, core: 2. Of those that a mesh axis runs over, the one named last changes fastest.
Arguments:
- hidden: bfloat16 [2048, 2304], P(('dp', 'cp')), parts along dimension 0
- positions: int32 [2048], P(('dp', 'cp')), parts along dimension 0
- w_q: bfloat16 [2, 2304, 2048], P(None, None, 'tp')
- w_k: bfloat16 [2, 2304, 1024], P(None, None, 'tp')
- w_v: bfloat16 [2, 2304, 1024], P(None, None, 'tp')
- w_o: bfloat16 [2, 2048, 2304], P(None, 'tp')
- w_gate: bfloat16 [2, 2304, 9216], P(None, None, 'tp')
- w_up: bfloat16 [2, 2304, 9216], P(None, None, 'tp')
- w_down: bfloat16 [2, 9216, 2304], P(None, 'tp')
- norm_gain: float32 [2, 4, 2304], replicated
- qk_gain: float32 [2, 2, 256], replicated
Outputs:
- output 1: bfloat16 [2048, 2304], P(('dp', 'cp')), parts along dimension 0
- output 2: bfloat16 [2, 2048, 4, 256], P(None, ('dp', 'cp'), 'tp'), parts along dimension 1
- output 3: bfloat16 [2, 2048, 4, 256], P(None, ('dp', 'cp'), 'tp'), parts along dimension 1
There are 2 independent parts. A program takes and returns all parts, laid end to end along the dimension named above; an argument that names none is the same for every part.
All inputs are finite; a program needn't handle non-finite values.
Results may differ from a plain program's by a relative error of at most 0.0166709.
Values are sent between devices in bfloat16 or wider.
A program may use at most 1 GiB of HBM per device.

v0:
```python
import math
import jax
import jax.numpy as jnp
from jax import lax
from jax.sharding import PartitionSpec as P

WINDOW = 1024
THETAS = (10000.0, 1000000.0)
EPS = 1e-6
NEG_BIG = -1e30


def rms_scale(values, gain):
    mean_sq = jnp.mean(values * values, axis=-1, keepdims=True)
    return values * lax.rsqrt(mean_sq + EPS) * (1.0 + gain)


def rotary(values, positions, theta):
    head_dim = values.shape[-1]
    half_dim = head_dim // 2
    inv_freq = theta ** (-(jnp.arange(half_dim, dtype=jnp.float32) * 2.0) / head_dim)
    angles = positions.astype(jnp.float32)[..., None] * inv_freq
    cosine = jnp.cos(angles)[..., None, :]
    sine_val = jnp.sin(angles)[..., None, :]
    lower_half = values[..., :half_dim]
    upper_half = values[..., half_dim:]
    return jnp.concatenate([lower_half * cosine - upper_half * sine_val, upper_half * cosine + lower_half * sine_val], axis=-1)


def project_qkv(state_f, positions, w_q, w_k, w_v, layer_gain, qk_pair, theta, head_dim):
    normed = rms_scale(state_f, layer_gain[0]).astype(jnp.bfloat16)
    head_shape = normed.shape[:-1] + (-1, head_dim)
    q_proj = jnp.dot(normed, w_q, preferred_element_type=jnp.float32).reshape(head_shape)
    k_proj = jnp.dot(normed, w_k, preferred_element_type=jnp.float32).reshape(head_shape)
    v_rows = jnp.dot(normed, w_v, preferred_element_type=jnp.float32).astype(jnp.bfloat16).reshape(head_shape)
    q_rot = rotary(rms_scale(q_proj, qk_pair[0]), positions, theta).astype(jnp.bfloat16)
    k_rot = rotary(rms_scale(k_proj, qk_pair[1]), positions, theta).astype(jnp.bfloat16)
    return q_rot, k_rot, v_rows


def attend(queries, key_rows, val_rows, q_start, k_start, window, lo_block, hi_block, block_len):
    n_query, kv_local, groups, head_dim = queries.shape
    score_scale = head_dim ** -0.5
    query_index = q_start + jnp.arange(n_query)
    init_state = (
        jnp.full((kv_local, groups, n_query, 1), NEG_BIG, jnp.float32),
        jnp.zeros((kv_local, groups, n_query, 1), jnp.float32),
        jnp.zeros((kv_local, groups, n_query, head_dim), jnp.float32),
    )

    def loop_body(step_id, loop_state):
        run_max, run_sum, acc_out = loop_state
        key_blk = lax.dynamic_slice_in_dim(key_rows, step_id * block_len, block_len, 0)
        val_blk = lax.dynamic_slice_in_dim(val_rows, step_id * block_len, block_len, 0)
        scores = jnp.einsum('qhgd,uhd->hgqu', queries, key_blk, preferred_element_type=jnp.float32) * score_scale
        key_index = k_start + step_id * block_len + jnp.arange(block_len)
        distance = query_index[:, None] - key_index[None, :]
        allowed = (distance >= 0) & (distance < window) & (key_index >= 0)[None, :]
        scores = jnp.where(allowed, scores, NEG_BIG)
        new_max = jnp.maximum(run_max, jnp.max(scores, axis=-1, keepdims=True))
        prob_blk = jnp.exp(scores - new_max)
        factor = jnp.exp(run_max - new_max)
        run_sum = run_sum * factor + jnp.sum(prob_blk, axis=-1, keepdims=True)
        acc_out = acc_out * factor + jnp.einsum('hgqu,uhd->hgqd', prob_blk.astype(jnp.bfloat16), val_blk, preferred_element_type=jnp.float32)
        return new_max, run_sum, acc_out

    run_max, run_sum, acc_out = lax.fori_loop(lo_block, hi_block, loop_body, init_state)
    result = (acc_out / run_sum).astype(jnp.bfloat16)
    return jnp.transpose(result, (2, 0, 1, 3)).reshape(n_query, kv_local * groups * head_dim)


def finish_layer(state_f, attn_rows, w_o, w_gate, w_up, w_down, layer_gain):
    attn_out = lax.psum(jnp.dot(attn_rows, w_o, preferred_element_type=jnp.float32), 'tp')
    resid_f = (state_f + rms_scale(attn_out, layer_gain[1])).astype(jnp.bfloat16).astype(jnp.float32)
    normed = rms_scale(resid_f, layer_gain[2]).astype(jnp.bfloat16)
    gate_proj = jnp.dot(normed, w_gate, preferred_element_type=jnp.float32)
    up_proj = jnp.dot(normed, w_up, preferred_element_type=jnp.float32)
    act_rows = (jax.nn.gelu(gate_proj, approximate=True) * up_proj).astype(jnp.bfloat16)
    mlp_out = lax.psum(jnp.dot(act_rows, w_down, preferred_element_type=jnp.float32), 'tp')
    return (resid_f + rms_scale(mlp_out, layer_gain[3])).astype(jnp.bfloat16)


def solution(mesh):
    cp_size = mesh.shape['cp']
    row_spec = P(('dp', 'cp'), None)
    col_spec = P(None, None, 'tp')
    row_w_spec = P(None, 'tp', None)
    cache_spec = P(None, ('dp', 'cp'), 'tp', None)

    def device_fn(hidden, positions, w_q, w_k, w_v, w_o, w_gate, w_up, w_down, norm_gain, qk_gain):
        tok_rows = hidden.shape[0]
        head_dim = qk_gain.shape[-1]
        kv_local = w_k.shape[-1] // head_dim
        groups = w_q.shape[-1] // w_k.shape[-1]
        block_len = math.gcd(tok_rows, 256)
        q_start = lax.axis_index('cp') * tok_rows
        hi_block = (q_start + tok_rows) // block_len
        state_f = hidden.astype(jnp.float32)
        new_hidden = hidden
        k_list = []
        v_list = []
        for layer_id in range(2):
            q_rot, k_rot, v_rows = project_qkv(state_f, positions, w_q[layer_id], w_k[layer_id], w_v[layer_id], norm_gain[layer_id], qk_gain[layer_id], THETAS[layer_id], head_dim)
            k_all = lax.all_gather(k_rot, 'cp', axis=0, tiled=True)
            v_all = lax.all_gather(v_rows, 'cp', axis=0, tiled=True)
            if layer_id == 0:
                window = WINDOW
                lo_block = jnp.maximum(q_start - (WINDOW - 1), 0) // block_len
            else:
                window = tok_rows * cp_size
                lo_block = jnp.zeros((), jnp.int32)
            q_group = q_rot.reshape(tok_rows, kv_local, groups, head_dim)
            attn_rows = attend(q_group, k_all, v_all, q_start, 0, window, lo_block, hi_block, block_len)
            new_hidden = finish_layer(state_f, attn_rows, w_o[layer_id], w_gate[layer_id], w_up[layer_id], w_down[layer_id], norm_gain[layer_id])
            state_f = new_hidden.astype(jnp.float32)
            k_list.append(k_rot)
            v_list.append(v_rows)
        return new_hidden, jnp.stack(k_list), jnp.stack(v_list)

    return jax.shard_map(
        device_fn,
        mesh=mesh,
        in_specs=(row_spec, P(('dp', 'cp')), col_spec, col_spec, col_spec, row_w_spec, col_spec, col_spec, row_w_spec, P(), P()),
        out_specs=(row_spec, cache_spec, cache_spec),
        check_vma=False,
    )
```

profile of v0, /device:TPU:4, one launch (start us, length us, event | category | flops | bytes accessed | tf_op | source)
XLA Modules:
  0.0 534.5 jit_solution(3334688131655864683)
XLA Ops:
  7.2 1.3 add_reduce_fusion
  8.5 1.6 fusion.70
  10.1 4.1 slice_bitcast_fusion
  14.2 4.4 copy.25
  18.6 3.0 multiply_reduce_fusion.5
  21.7 1.8 multiply_cosine_fusion
  23.7 2.4 multiply_reduce_fusion.7
  26.2 0.6 fusion.155
  26.8 6.8 %all_gather.12 = bf16[1024,1,256]{0,2,1:T(8,128)(2,1)} all-gather(bf16[256,1,256]{0,2,1:T(8,128)(2,1)S(1)} %pad_maximum_fusion.3), channel_id=1, replica_groups=mesh['dp'=2,'tp'=4,'cp'=4] {'cp'}, dimensions={0}, use_global_device_ids=true | all-gather | bytes 655360 | tf_op jit(solution)/shard_map/all_gather | solution.py:104
  33.6 2.1 fusion.130
  35.7 7.2 %all-gather = bf16[1024,256]{1,0:T(8,128)(2,1)} all-gather(bf16[256,256]{1,0:T(8,128)(2,1)S(1)} %fusion.130), channel_id=2, replica_groups=mesh['dp'=2,'tp'=4,'cp'=4] {'cp'}, dimensions={0}, use_global_device_ids=true | all-gather | bytes 655360 | tf_op jit(solution)/shard_map/all_gather | solution.py:105
  43.0 8.6 %while.30 = (s32[]{:T(128)}, f32[1,2,256,1]{2,1,3,0:T(2,128)S(1)}, f32[1,2,256,1]{2,1,3,0:T(2,128)S(1)}, f32[1,2,256,256]{3,2,1,0:T(8,128)S(1)}, s32[]{:T(128)},...) while((s32[]{:T(128)}, f32[1,2,256,1]{2,1,3,0:T(2,128)S(1)}, ...), condition=%wide.region_6.7_spmd.clone, body=%wide.region_3.6_spmd.clone.sunk | while | flops 135727616 | bytes 3314367 | solution.py:67
  43.2 1.2 fusion.195
  44.4 1.3 fusion.198
  46.1 1.2 fusion.195
  47.3 1.3 fusion.198
  48.9 1.2 fusion.195
  50.1 1.3 fusion.198
  51.6 1.0 copy.28
  52.6 1.1 divide_convert_fusion.1
  53.7 3.9 fusion.106
  57.8 98.1 %all-reduce.5.cloned.1.call-done = f32[256,2304]{1,0:T(8,128)} async-done(((f32[256,2304]{1,0:T(8,128)}), f32[256,2304]{1,0:T(8,128)}) %all-reduce.5.cloned.1.call-update) | async-done | bytes 2359312 | tf_op jit(solution)/shard_map/psum | solution.py:73
  155.9 2.1 multiply_reduce_fusion.3
  158.3 1.9 fusion.74
  160.3 1.0 copy-done.4
  161.3 8.6 %fusion.84 = f32[256,2304]{1,0:T(8,128)} fusion(bf16[2,2304,2304]{2,1,0:T(8,128)(2,1)} %param.21, bf16[256,2304]{1,0:T(8,128)(2,1)S(1)} %get-tuple-element.244, f32[2304]{0:T(1024)S(1)} %get-tuple-element.195, f32[256]{0:T(256)S(1)} %add_rsqrt_fusion.8), kind=kOutput, calls=%fused_computation.108 | convolution fusion | flops 2724986880 | bytes 14166016 | tf_op jit(solution)/shard_map/dot_general | solution.py:76
  169.8 15.3 %fusion.46 = f32[256,2304]{1,0:T(8,128)} fusion(bf16[2,2304,2304]{2,1,0:T(8,128)(2,1)} %param.23, f32[256,2304]{1,0:T(8,128)} %fusion.84, bf16[2,2304,2304]{2,1,0:T(8,128)(2,1)} %param.22, bf16[256,2304]{1,0:T(8,128)(2,1)} %copy-done.4, f32[2304]{0:T(1024)S(1)} %get-tuple-element.195, f32[256]{0:T(256)S(1)} %add_rsqrt_fusion.8), kind=kOutput, calls=%fused_computation.64 | convolution fusion | flops 5439356928 | bytes 27142144 | tf_op jit(solution)/shard_map/dot_general | solution.py:79
  185.2 2.6 copy.29
  187.8 91.0 %all-reduce.7.cloned.1.call-done = f32[256,2304]{1,0:T(8,128)} async-done(((f32[256,2304]{1,0:T(8,128)}), f32[256,2304]{1,0:T(8,128)}) %all-reduce.7.cloned.1.call-update) | async-done | bytes 2359312 | tf_op jit(solution)/shard_map/psum | solution.py:79
  278.9 2.1 multiply_reduce_fusion.2
  281.2 2.1 fusion.87
  283.4 0.8 multiply_reduce_fusion.6
  284.1 0.9 copy-done.15
  286.3 6.7 %all-gather.1 = bf16[1024,256]{1,0:T(8,128)(2,1)S(1)} all-gather(bf16[256,256]{1,0:T(8,128)(2,1)S(1)} %fusion.133), channel_id=3, replica_groups=mesh['dp'=2,'tp'=4,'cp'=4] {'cp'}, dimensions={0}, use_global_device_ids=true | all-gather | bytes 655360 | tf_op jit(solution)/shard_map/all_gather | solution.py:105
  293.0 0.9 multiply_reduce_fusion.4
  294.3 7.3 %all_gather.14 = bf16[1024,1,256]{0,2,1:T(8,128)(2,1)S(1)} all-gather(bf16[256,1,256]{0,2,1:T(8,128)(2,1)S(1)} %pad_maximum_fusion.4), channel_id=1, replica_groups=mesh['dp'=2,'tp'=4,'cp'=4] {'cp'}, dimensions={0}, use_global_device_ids=true | all-gather | bytes 655360 | tf_op jit(solution)/shard_map/all_gather | solution.py:104
  301.7 3.2 while.31
  305.1 3.9 fusion.104
  309.0 94.8 %all-reduce.9.cloned.1.call-done = f32[256,2304]{1,0:T(8,128)} async-done(((f32[256,2304]{1,0:T(8,128)}), f32[256,2304]{1,0:T(8,128)}) %all-reduce.9.cloned.1.call-update) | async-done | bytes 2359312 | tf_op jit(solution)/shard_map/psum | solution.py:73
  403.8 2.1 multiply_reduce_fusion.1
  406.2 0.7 fusion.91
  406.9 8.6 %fusion.101 = f32[256,2304]{1,0:T(8,128)} fusion(bf16[2,2304,2304]{2,1,0:T(8,128)(2,1)} %param.21, bf16[256,2304]{1,0:T(8,128)(2,1)S(1)} %get-tuple-element.240, f32[2304]{0:T(1024)S(1)} %get-tuple-element.198, f32[256]{0:T(256)S(1)} %add_rsqrt_fusion.3), kind=kOutput, calls=%fused_computation.123 | convolution fusion | flops 2724986880 | bytes 14166016 | tf_op jit(solution)/shard_map/dot_general | solution.py:76
  415.4 15.0 %fusion.40 = f32[256,2304]{1,0:T(8,128)} fusion(bf16[2,2304,2304]{2,1,0:T(8,128)(2,1)} %param.23, f32[256,2304]{1,0:T(8,128)} %fusion.101, bf16[2,2304,2304]{2,1,0:T(8,128)(2,1)} %param.22, bf16[256,2304]{1,0:T(8,128)(2,1)S(1)} %get-tuple-element.240, f32[2304]{0:T(1024)S(1)} %get-tuple-element.198, f32[256]{0:T(256)S(1)} %add_rsqrt_fusion.3), kind=kOutput, calls=%fused_computation.58 | convolution fusion | flops 5439356928 | bytes 27142144 | tf_op jit(solution)/shard_map/dot_general | solution.py:79
  430.5 0.8 copy.33
  431.4 0.7 pad_maximum_fusion.2
  432.1 92.0 %all-reduce.11.cloned.1.call-done = f32[256,2304]{1,0:T(8,128)} async-done(((f32[256,2304]{1,0:T(8,128)}), f32[256,2304]{1,0:T(8,128)}) %all-reduce.11.cloned.1.call-update) | async-done | bytes 2359312 | tf_op jit(solution)/shard_map/psum | solution.py:79
  524.1 2.1 multiply_reduce_fusion
  526.5 1.5 fusion.94
  (124 shorter events, 8.0 us)
Async XLA Ops:
  7.2 148.8 %all-reduce.5.cloned.1.call-start = ((), (), s32[]{:S(2)}) async-start(), calls=%async_computation | async-start | bytes 4718592 | tf_op jit(solution)/shard_map/psum | solution.py:73
  18.6 3.0 copy-start.12
  18.6 3.0 copy-start.13
  35.7 7.2 %copy-start.6 = (bf16[256,256]{1,0:T(8,128)(2,1)}, bf16[256,256]{1,0:T(8,128)(2,1)S(1)}, u32[]{:S(2)}) copy-start(bf16[256,256]{1,0:T(8,128)(2,1)S(1)} %fusion.130) | copy-start | bytes 393220
  57.6 221.3 %all-reduce.7.cloned.1.call-start = ((), (), s32[]{:S(2)}) async-start(), calls=%async_computation.1 | async-start | bytes 4718592 | tf_op jit(solution)/shard_map/psum | solution.py:79
  155.9 2.4 copy-start.2
  160.2 1.0 copy-start.4
  185.2 218.6 %all-reduce.9.cloned.1.call-start = ((), (), s32[]{:S(2)}) async-start(), calls=%async_computation.2 | async-start | bytes 4718592 | tf_op jit(solution)/shard_map/psum | solution.py:73
  278.9 2.4 copy-start
  281.2 2.1 copy-start.14
  283.3 1.7 copy-start.15
  285.0 8.0 %copy-start.5 = (bf16[512,2304]{1,0:T(8,128)(2,1)S(1)}, bf16[512,2304]{1,0:T(8,128)(2,1)}, u32[]{:S(2)}) copy-start(bf16[512,2304]{1,0:T(8,128)(2,1)} %copy.29) | copy-start | bytes 7077892
  285.5 7.4 %copy-start.8 = (bf16[256,256]{1,0:T(8,128)(2,1)}, bf16[256,256]{1,0:T(8,128)(2,1)S(1)}, u32[]{:S(2)}) copy-start(bf16[256,256]{1,0:T(8,128)(2,1)S(1)} %fusion.133) | copy-start | bytes 393220
  293.0 1.1 copy-start.10
  293.0 1.1 copy-start.11
  309.0 215.2 %all-reduce.11.cloned.1.call-start = ((), (), s32[]{:S(2)}) async-start(), calls=%async_computation.3 | async-start | bytes 4718592 | tf_op jit(solution)/shard_map/psum | solution.py:79
  403.8 2.4 copy-start.1
  430.4 0.9 copy-start.7
  430.4 1.0 copy-start.9
  524.1 2.4 copy-start.3
Sparse Core Ops, SparseCore 0:
  57.7 98.1 all-reduce.4
  185.3 93.5 all-reduce.6
  309.1 94.6 all-reduce.8
  430.6 93.5 all-reduce.10
where the time goes:
time: 537 us; the launch traced here: 535 us
  waiting for transfers between devices  376 us (70%)
  matrix products  74.5 us (14%)
  blocking collectives  28 us (5%)
  other arithmetic  24.3 us (5%)
  local copies, waits for them, and re-layouts  16.7 us (3%)
  between operations  14.1 us (3%)
    psum x2, waiting for transfers between devices, finish_layer(): lax.psum(jnp.dot(attn_rows, w_o, preferred_element_type=jnp.float32), 'tp')  193 us
    psum x2, waiting for transfers between devices, finish_layer(): lax.psum(jnp.dot(act_rows, w_down, preferred_element_type=jnp.float32), '...  183 us
    dot_general x2, matrix products, finish_layer(): jnp.dot(act_rows, w_down, preferred_element_type=jnp.float32)  30.3 us
    dot_general x2, matrix products, finish_layer(): gate_proj = jnp.dot(normed, w_gate, preferred_element_type=jnp.float32)  17.2 us
    reduce_sum x8, other arithmetic, rms_scale(): mean_sq = jnp.mean(values * values, axis=-1, keepdims=True)  14.5 us
    all_gather x2, blocking collectives, device_fn(): k_all = lax.all_gather(k_rot, 'cp', axis=0, tiled=True)  14.1 us
    all_gather x2, blocking collectives, device_fn(): v_all = lax.all_gather(v_rows, 'cp', axis=0, tiled=True)  14 us
    dot_general x3, local copies, waits for them, and re-layouts, project_qkv(): jnp.dot(normed, w_q, preferred_element_type=jnp.float32).reshape(head_shape)  11.1 us
  transfers between devices with their start and end apart: 4, of which 4 were waited for; matrix products, arithmetic and copies ran while one was open for 1% of the time, Pallas kernels for 0%

commit v1 on v0

v1 whole, which is shorter than its diff:
```python
import functools
import jax
import jax.numpy as jnp
from jax import lax
from jax.experimental import pallas as pl
from jax.experimental.pallas import tpu as pltpu
from jax.sharding import PartitionSpec as P

MESH = pl.DeviceIdType.MESH
THETAS = (10000.0, 1000000.0)
EPS = 1e-6
NEG_BIG = -1e30
TOK = 256
D = 2304
HEAD = 256
HALF = 128
Q_HEADS = 2
FT = 256
NFT = D // FT
RS = 8
NRS = 128 // RS
AG = 16
NAG = 128 // AG
F32 = jnp.float32
BF16 = jnp.bfloat16


def norm_rows(src, gain, dst, rows=16):
    def body(i, carry):
        sl = pl.ds(pl.multiple_of(i * rows, rows), rows)
        vals = src[sl, :].astype(F32)
        mean_sq = jnp.mean(vals * vals, axis=-1, keepdims=True)
        dst[sl, :] = (vals * lax.rsqrt(mean_sq + EPS) * gain).astype(BF16)
        return carry

    lax.fori_loop(0, TOK // rows, body, 0)


def head_norm_rope(vals, gain, cosine, sine):
    mean_sq = jnp.mean(vals * vals, axis=-1, keepdims=True)
    vals = vals * lax.rsqrt(mean_sq + EPS) * gain
    low, high = vals[:, :HALF], vals[:, HALF:]
    return jnp.concatenate([low * cosine - high * sine, high * cosine + low * sine], axis=-1).astype(BF16)


def reduce_norm_share(z, part, land, res, gain, out, sems):
    rs_send, rs_recv, ag_send, ag_recv = sems

    def towards(flow):
        return z + 1 if flow else z - 1

    def away(flow):
        return z - 1 if flow else z + 1

    def rs_copy(flow, c):
        rows = pl.ds(pl.multiple_of(128 * flow + c * RS, RS), RS)
        return pltpu.make_async_remote_copy(
            src_ref=part.at[rows], dst_ref=land.at[rows], send_sem=rs_send.at[flow, c],
            recv_sem=rs_recv.at[flow, c], device_id={'tp': towards(flow)}, device_id_type=MESH)

    def ag_copy(flow, c):
        rows = pl.ds(pl.multiple_of(128 * flow + c * AG, AG), AG)
        return pltpu.make_async_remote_copy(
            src_ref=out.at[rows], dst_ref=out.at[rows], send_sem=ag_send.at[flow, c],
            recv_sem=ag_recv.at[flow, c], device_id={'tp': away(flow)}, device_id_type=MESH)

    def take(flow, c):
        rs_copy(flow, c).wait_recv()
        rows = pl.ds(pl.multiple_of(128 * flow + c * RS, RS), RS)
        part[rows, :] = part[rows, :] + land[rows, :]

    def hop(flow, c):
        take(flow, c)
        rs_copy(flow, c).start()

    def relay(flow, c):
        ag_copy(flow, c).wait_recv()
        ag_copy(flow, c).start()

    def loop(n, fn, start=0):
        def body(i, carry):
            fn(i)
            return carry
        lax.fori_loop(start, n, body, 0)

    def end_role(source, final):
        loop(NRS, lambda c: rs_copy(source, c).start())

        def finish(c):
            for i in range(AG // RS):
                take(final, c * (AG // RS) + i)
            rows = pl.ds(pl.multiple_of(128 * final + c * AG, AG), AG)
            vals = part[rows, :]
            mean_sq = jnp.mean(vals * vals, axis=-1, keepdims=True)
            out[rows, :] = (res[rows, :].astype(F32) + vals * lax.rsqrt(mean_sq + EPS) * gain).astype(BF16)
            ag_copy(final, c).start()

        loop(NAG, finish)
        loop(NAG, lambda c: ag_copy(source, c).wait_recv())
        loop(NRS, lambda c: rs_copy(source, c).wait_send())
        loop(NAG, lambda c: ag_copy(final, c).wait_send())

    def mid_role(near, far):
        hop(near, 0)

        def both(c):
            hop(near, c)
            hop(far, c - 1)

        loop(NRS, both, 1)
        hop(far, NRS - 1)

        def both_ag(c):
            relay(far, c)
            relay(near, c)

        loop(NAG, both_ag)
        loop(NRS, lambda c: rs_copy(near, c).wait_send())
        loop(NRS, lambda c: rs_copy(far, c).wait_send())
        loop(NAG, lambda c: ag_copy(near, c).wait_send())
        loop(NAG, lambda c: ag_copy(far, c).wait_send())

    pl.when(z == 0)(lambda: end_role(1, 0))
    pl.when(z == 1)(lambda: mid_role(1, 0))
    pl.when(z == 2)(lambda: mid_role(0, 1))
    pl.when(z == 3)(lambda: end_role(0, 1))


def layer_kernel(layer, x_ref, rope_ref, wq_hbm, wk_hbm, wv_hbm, wo_hbm, wg_hbm, wu_hbm, wd_hbm, gain_ref, qk_ref,
                 x_out, k_out, v_out,
                 wq, wk, wv, wo, wg, wu, wd, h_buf, r_buf, s_buf, part, land, q_buf, kv, acc, run_max, run_sum,
                 w_sem, t_sem, kv_send, kv_recv, rs_send, rs_recv, ag_send, ag_recv):
    z = lax.axis_index('tp')
    me = lax.axis_index('cp')
    twin = me + 1 - 2 * lax.rem(me, 2)
    across = lax.rem(me + 2, 4)

    barrier = pltpu.get_barrier_semaphore()
    pl.when(z > 0)(lambda: pl.semaphore_signal(barrier, inc=1, device_id={'tp': z - 1}, device_id_type=MESH))
    pl.when(z < 3)(lambda: pl.semaphore_signal(barrier, inc=1, device_id={'tp': z + 1}, device_id_type=MESH))
    pl.semaphore_signal(barrier, inc=1, device_id={'cp': twin}, device_id_type=MESH)
    pl.semaphore_signal(barrier, inc=1, device_id={'cp': across}, device_id_type=MESH)

    loads = [pltpu.make_async_copy(src.at[layer], dst, w_sem.at[i])
             for i, (src, dst) in enumerate(((wk_hbm, wk), (wv_hbm, wv), (wq_hbm, wq), (wo_hbm, wo)))]
    for copy in loads:
        copy.start()

    def tile_load(kind, src, dst, t):
        cols = pl.ds(pl.multiple_of(t * FT, FT), FT)
        return pltpu.make_async_copy(src.at[layer, :, cols], dst.at[t], t_sem.at[kind, t])

    def start_gate_up(t, carry):
        tile_load(0, wg_hbm, wg, t).start()
        tile_load(1, wu_hbm, wu, t).start()
        return carry

    def start_down(t, carry):
        tile_load(2, wd_hbm, wd, t).start()
        return carry

    lax.fori_loop(0, NFT, start_gate_up, 0)
    lax.fori_loop(0, NFT, start_down, 0)

    gains = [1.0 + gain_ref[layer, i:i + 1, :] for i in range(4)]
    q_gain = 1.0 + qk_ref[layer, 0:1, :]
    k_gain = 1.0 + qk_ref[layer, 1:2, :]
    cosine, sine = rope_ref[layer, 0], rope_ref[layer, 1]

    norm_rows(x_ref, gains[0], h_buf)
    state = h_buf[...]

    loads[0].wait()
    k_rot = head_norm_rope(jnp.dot(state, wk[...], preferred_element_type=F32), k_gain, cosine, sine)
    kv[me, 0] = k_rot
    k_out[...] = k_rot
    loads[1].wait()
    v_rows = jnp.dot(state, wv[...], preferred_element_type=F32).astype(BF16)
    kv[me, 1] = v_rows
    v_out[...] = v_rows

    near_count = jnp.where(z > 0, 1, 0) + jnp.where(z < 3, 1, 0)
    pl.semaphore_wait(barrier, near_count + 2)

    def kv_copy(slot, part_id, lane, target):
        return pltpu.make_async_remote_copy(
            src_ref=kv.at[slot, part_id], dst_ref=kv.at[slot, part_id], send_sem=kv_send.at[lane, part_id],
            recv_sem=kv_recv.at[slot, part_id], device_id={'cp': target}, device_id_type=MESH)

    def send_own():
        for i in range(2):
            pl.when(me < 2)(lambda: kv_copy(me, i, 1, across).start())
            pl.when(lax.rem(me, 2) == 0)(lambda: kv_copy(me, i, 0, twin).start())

    send_own()

    loads[2].wait()
    q_all = jnp.dot(state, wq[...], preferred_element_type=F32)
    for i in range(Q_HEADS):
        q_buf[i * TOK:(i + 1) * TOK, :] = head_norm_rope(
            q_all[:, i * HEAD:(i + 1) * HEAD], q_gain, cosine, sine)

    def scores_of(slot):
        return lax.dot_general(q_buf[...], kv[slot, 0], (((1,), (1,)), ((), ())),
                               preferred_element_type=F32) * (HEAD ** -0.5)

    def first_block():
        scores = scores_of(me)
        row = lax.broadcasted_iota(jnp.int32, (Q_HEADS, TOK, TOK), 1).reshape(Q_HEADS * TOK, TOK)
        col = lax.broadcasted_iota(jnp.int32, (Q_HEADS * TOK, TOK), 1)
        scores = jnp.where(row >= col, scores, NEG_BIG)
        top = jnp.max(scores, axis=-1, keepdims=True)
        prob = jnp.exp(scores - top)
        run_max[...] = jnp.broadcast_to(top, run_max.shape)
        run_sum[...] = jnp.broadcast_to(jnp.sum(prob, axis=-1, keepdims=True), run_sum.shape)
        acc[...] = jnp.dot(prob.astype(BF16), kv[me, 1], preferred_element_type=F32)

    def next_block(slot):
        scores = scores_of(slot)
        old = run_max[:, :1]
        top = jnp.maximum(old, jnp.max(scores, axis=-1, keepdims=True))
        prob = jnp.exp(scores - top)
        factor = jnp.exp(old - top)
        run_max[...] = jnp.broadcast_to(top, run_max.shape)
        run_sum[...] = run_sum[...] * factor + jnp.sum(prob, axis=-1, keepdims=True)
        acc[...] = acc[...] * factor + jnp.dot(prob.astype(BF16), kv[slot, 1], preferred_element_type=F32)

    first_block()

    def recv(slot):
        for i in range(2):
            kv_copy(slot, i, 0, twin).wait_recv()

    def relay(slot):
        for i in range(2):
            kv_copy(slot, i, 0, twin).wait_recv()
            kv_copy(slot, i, 2, twin).start()

    def sent(lane, slot):
        for i in range(2):
            kv_copy(slot, i, lane, twin).wait_send()

    @pl.when(me == 0)
    def _():
        sent(0, 0)
        sent(1, 0)

    @pl.when(me == 1)
    def _():
        recv(0)
        next_block(0)
        sent(1, 1)

    @pl.when(me == 2)
    def _():
        relay(0)
        next_block(0)
        recv(1)
        next_block(1)
        sent(0, 2)
        sent(2, 0)

    @pl.when(me == 3)
    def _():
        recv(2)
        next_block(2)
        relay(1)
        next_block(1)
        recv(0)
        next_block(0)
        sent(2, 1)

    loads[3].wait()
    for i in range(Q_HEADS):
        rows = slice(i * TOK, (i + 1) * TOK)
        s_buf[:, i * HEAD:(i + 1) * HEAD] = (acc[rows, :] / run_sum[rows, :1]).astype(BF16)
    part[...] = jnp.dot(s_buf[:, :Q_HEADS * HEAD], wo[...], preferred_element_type=F32)

    def phase(n):
        return (rs_send.at[n], rs_recv.at[n], ag_send.at[n], ag_recv.at[n])

    reduce_norm_share(z, part, land, x_ref, gains[1], r_buf, phase(0))

    norm_rows(r_buf, gains[2], h_buf)

    def gate_up(t, carry):
        tile_load(0, wg_hbm, wg, t).wait()
        tile_load(1, wu_hbm, wu, t).wait()
        gate = jnp.dot(h_buf[...], wg[t], preferred_element_type=F32)
        up = jnp.dot(h_buf[...], wu[t], preferred_element_type=F32)
        s_buf[:, pl.ds(pl.multiple_of(t * FT, FT), FT)] = (jax.nn.gelu(gate, approximate=True) * up).astype(BF16)
        return carry

    lax.fori_loop(0, NFT, gate_up, 0)

    def down(t, carry):
        tile_load(2, wd_hbm, wd, t).wait()
        part[:, pl.ds(pl.multiple_of(t * FT, FT), FT)] = jnp.dot(s_buf[...], wd[t], preferred_element_type=F32)
        return carry

    lax.fori_loop(0, NFT, down, 0)

    reduce_norm_share(z, part, land, r_buf, gains[3], x_out, phase(1))


def run_layer(layer, x, rope, weights, norm_gain, qk_gain):
    vmem = pl.BlockSpec(memory_space=pltpu.VMEM)
    hbm = pl.BlockSpec(memory_space=pl.ANY)
    sem = pltpu.SemaphoreType.DMA
    return pl.pallas_call(
        functools.partial(layer_kernel, layer),
        name=f'layer_{layer}',
        out_shape=(
            jax.ShapeDtypeStruct((TOK, D), BF16),
            jax.ShapeDtypeStruct((TOK, HEAD), BF16),
            jax.ShapeDtypeStruct((TOK, HEAD), BF16),
        ),
        in_specs=[vmem, vmem] + [hbm] * 7 + [vmem, vmem],
        out_specs=(vmem, vmem, vmem),
        scratch_shapes=[
            pltpu.VMEM((D, Q_HEADS * HEAD), BF16),
            pltpu.VMEM((D, HEAD), BF16),
            pltpu.VMEM((D, HEAD), BF16),
            pltpu.VMEM((Q_HEADS * HEAD, D), BF16),
            pltpu.VMEM((NFT, D, FT), BF16),
            pltpu.VMEM((NFT, D, FT), BF16),
            pltpu.VMEM((NFT, D, FT), BF16),
            pltpu.VMEM((TOK, D), BF16),
            pltpu.VMEM((TOK, D), BF16),
            pltpu.VMEM((TOK, D), BF16),
            pltpu.VMEM((TOK, D), F32),
            pltpu.VMEM((TOK, D), F32),
            pltpu.VMEM((Q_HEADS * TOK, HEAD), BF16),
            pltpu.VMEM((4, 2, TOK, HEAD), BF16),
            pltpu.VMEM((Q_HEADS * TOK, HEAD), F32),
            pltpu.VMEM((Q_HEADS * TOK, 128), F32),
            pltpu.VMEM((Q_HEADS * TOK, 128), F32),
            sem((4,)),
            sem((3, NFT)),
            sem((3, 2)),
            sem((4, 2)),
            sem((2, 2, NRS)),
            sem((2, 2, NRS)),
            sem((2, 2, NAG)),
            sem((2, 2, NAG)),
        ],
        compiler_params=pltpu.CompilerParams(
            collective_id=layer, has_side_effects=True, vmem_limit_bytes=67043328),
    )(x, rope, *weights, norm_gain, qk_gain)


def solution(mesh):
    row_spec = P(('dp', 'cp'), None)
    col_spec = P(None, None, 'tp')
    row_w_spec = P(None, 'tp', None)
    cache_spec = P(None, ('dp', 'cp'), 'tp', None)

    def device_fn(hidden, positions, w_q, w_k, w_v, w_o, w_gate, w_up, w_down, norm_gain, qk_gain):
        pos = positions.astype(F32)[:, None]
        exponent = -(jnp.arange(HALF, dtype=F32) * 2.0) / HEAD
        angles = jnp.stack([pos * (theta ** exponent) for theta in THETAS])
        rope = jnp.stack([jnp.cos(angles), jnp.sin(angles)], axis=1)
        weights = (w_q, w_k, w_v, w_o, w_gate, w_up, w_down)
        x1, k0, v0 = run_layer(0, hidden, rope, weights, norm_gain, qk_gain)
        x2, k1, v1 = run_layer(1, x1, rope, weights, norm_gain, qk_gain)
        return x2, jnp.stack([k0, k1])[:, :, None, :], jnp.stack([v0, v1])[:, :, None, :]

    return jax.shard_map(
        device_fn,
        mesh=mesh,
        in_specs=(row_spec, P(('dp', 'cp')), col_spec, col_spec, col_spec, row_w_spec, col_spec, col_spec, row_w_spec, P(), P()),
        out_specs=(row_spec, cache_spec, cache_spec),
        check_vma=False,
    )
```

time: 537 us -> 335 us (0.62)
  waiting for transfers between devices: 376 us -> 0 us
  Pallas kernels: 0 us -> 326 us
  matrix products: 74.5 us -> 0 us
  blocking collectives: 28 us -> 0 us
  other arithmetic: 24.3 us -> 5.98 us
  local copies, waits for them, and re-layouts: 16.7 us -> 2.36 us
  between operations: 14.1 us -> 0.66 us
    psum x4 -> x0, waiting for transfers between devices: 376 us -> none  [the longest x2 193 us: finish_layer(): lax.psum(jnp.dot(attn_rows, w_o, preferred_element_type=jnp.float32), 'tp')]
    pallas_call x0 -> x2, Pallas kernels: none -> 326 us  [run_layer(): pl.pallas_call(functools.partial(layer_kernel, layer), name=f'layer_{laye...]
    dot_general x24 -> x0, matrix products: 74.5 us -> none  [the longest x2 30.3 us: finish_layer(): jnp.dot(act_rows, w_down, preferred_element_type=jnp.float32)]
    all_gather x4 -> x0, blocking collectives: 28 us -> none  [the longest x2 14.1 us: device_fn(): k_all = lax.all_gather(k_rot, 'cp', axis=0, tiled=True)]
    reduce_sum x14 -> x0, other arithmetic: 15 us -> none  [the longest x8 14.5 us: rms_scale(): mean_sq = jnp.mean(values * values, axis=-1, keepdims=True)]
    dot_general x3 -> x0, local copies, waits for them, and re-layouts: 11.1 us -> none  [project_qkv(): jnp.dot(normed, w_q, preferred_element_type=jnp.float32).reshape(head_shape)]
  transfers between devices with their start and end apart: 4 -> 0, of which waited for: 4 -> 0; matrix products, arithmetic and copies ran while one was open for 1% -> 0% of each run, Pallas kernels for 0% -> 0%
where the time goes in v1:
time: 335 us
  Pallas kernels  326 us (97%)
  other arithmetic  5.98 us (2%)
    pallas_call x2, Pallas kernels, run_layer(): pl.pallas_call(functools.partial(layer_kernel, layer), name=f'layer_{laye...  326 us

profile of v1, /device:TPU:4, one launch (start us, length us, event | category | flops | bytes accessed | tf_op | source)
XLA Modules:
  0.0 334.8 jit_solution(4090111032167787021)
XLA Ops:
  0.6 0.7 convert_element_type.3
  1.3 0.1 multiply_bitcast_fusion.1
  1.4 1.0 fusion.1
  2.4 0.8 pad_maximum_fusion.rope_ref
  3.2 165.2 %layer_0.1 = (bf16[256,2304]{1,0:T(8,128)(2,1)}, bf16[256,256]{1,0:T(8,128)(2,1)}, bf16[256,256]{1,0:T(8,128)(2,1)}) custom-call(bf16[256,2304]{1,0:T(8,128)(2,1)} %x_ref.1, f32[2,2,256,128]{3,2,1,0:T(8,128)} %pad_maximum_fusion.rope_ref, bf16[2,2304,512]{2,1,0:T(8,128)(2,1)} %wq_hbm.3, bf16[2,2304,256]{2,1,0:T(8,128)(2,1)} %wk_hbm.3, ...), custom_call_target="tpu_custom_call" | custom-call | tf_op jit(solution)/shard_map/layer_0/pallas_call | solution.py:310
  168.5 160.6 %layer_1.1 = (bf16[256,2304]{1,0:T(8,128)(2,1)}, bf16[256,256]{1,0:T(8,128)(2,1)}, bf16[256,256]{1,0:T(8,128)(2,1)}) custom-call(bf16[256,2304]{1,0:T(8,128)(2,1)} %get-tuple-element.9.x_ref, f32[2,2,256,128]{3,2,1,0:T(8,128)} %pad_maximum_fusion.rope_ref, bf16[2,2304,512]{2,1,0:T(8,128)(2,1)} %wq_hbm.3, bf16[2,2304,256]{2,1,0:T(8,128)(2,1)} %wk_hbm.3, ...), custom_call_target="tpu_custom_call" | custom-call | tf_op jit(solution)/shard_map/layer_1/pallas_call | solution.py:310
  329.1 1.7 maximum_bitcast_fusion
  330.8 1.7 maximum_bitcast_fusion.1
  332.5 2.4 copy.17
  (1 shorter events, 0.0 us)

commit v2 on v1

--- a/solution.py
+++ b/solution.py
@@ -1,6 +1,7 @@
 import functools
 import jax
 import jax.numpy as jnp
+import numpy as np
 from jax import lax
 from jax.experimental import pallas as pl
 from jax.experimental.pallas import tpu as pltpu
@@ -21,6 +22,8 @@
 NRS = 128 // RS
 AG = 16
 NAG = 128 // AG
+RS_LAG = 4
+AG_LAG = 4
 F32 = jnp.float32
 BF16 = jnp.bfloat16
 
@@ -101,20 +104,18 @@
         loop(NAG, lambda c: ag_copy(final, c).wait_send())
 
     def mid_role(near, far):
-        hop(near, 0)
-
-        def both(c):
-            hop(near, c)
-            hop(far, c - 1)
-
-        loop(NRS, both, 1)
-        hop(far, NRS - 1)
-
-        def both_ag(c):
-            relay(far, c)
-            relay(near, c)
-
-        loop(NAG, both_ag)
+        def lagged(n, lag, first, second):
+            loop(lag, first)
+
+            def both(c):
+                first(c)
+                second(c - lag)
+
+            loop(n, both, lag)
+            loop(n, second, n - lag)
+
+        lagged(NRS, RS_LAG, lambda c: hop(near, c), lambda c: hop(far, c))
+        lagged(NAG, AG_LAG, lambda c: relay(far, c), lambda c: relay(near, c))
         loop(NRS, lambda c: rs_copy(near, c).wait_send())
         loop(NRS, lambda c: rs_copy(far, c).wait_send())
         loop(NAG, lambda c: ag_copy(near, c).wait_send())
@@ -126,7 +127,7 @@
     pl.when(z == 3)(lambda: end_role(0, 1))
 
 
-def layer_kernel(layer, x_ref, rope_ref, wq_hbm, wk_hbm, wv_hbm, wo_hbm, wg_hbm, wu_hbm, wd_hbm, gain_ref, qk_ref,
+def layer_kernel(layer, x_ref, cos_ref, sin_ref, wq_hbm, wk_hbm, wv_hbm, wo_hbm, wg_hbm, wu_hbm, wd_hbm, gain_ref, qk_ref,
                  x_out, k_out, v_out,
                  wq, wk, wv, wo, wg, wu, wd, h_buf, r_buf, s_buf, part, land, q_buf, kv, acc, run_max, run_sum,
                  w_sem, t_sem, kv_send, kv_recv, rs_send, rs_recv, ag_send, ag_recv):
@@ -165,7 +166,7 @@
     gains = [1.0 + gain_ref[layer, i:i + 1, :] for i in range(4)]
     q_gain = 1.0 + qk_ref[layer, 0:1, :]
     k_gain = 1.0 + qk_ref[layer, 1:2, :]
-    cosine, sine = rope_ref[layer, 0], rope_ref[layer, 1]
+    cosine, sine = cos_ref[layer], sin_ref[layer]
 
     norm_rows(x_ref, gains[0], h_buf)
     state = h_buf[...]
@@ -315,7 +316,7 @@
             jax.ShapeDtypeStruct((TOK, HEAD), BF16),
             jax.ShapeDtypeStruct((TOK, HEAD), BF16),
         ),
-        in_specs=[vmem, vmem] + [hbm] * 7 + [vmem, vmem],
+        in_specs=[vmem] * 3 + [hbm] * 7 + [vmem, vmem],
         out_specs=(vmem, vmem, vmem),
         scratch_shapes=[
             pltpu.VMEM((D, Q_HEADS * HEAD), BF16),
@@ -346,7 +347,28 @@
         ],
         compiler_params=pltpu.CompilerParams(
             collective_id=layer, has_side_effects=True, vmem_limit_bytes=67043328),
-    )(x, rope, *weights, norm_gain, qk_gain)
+    )(x, *rope, *weights, norm_gain, qk_gain)
+
+
+def pack_kernel(x_in, k0, k1, v0, v1, x_out, k_out, v_out, sem):
+    copies = [pltpu.make_async_copy(src, dst, sem.at[i]) for i, (src, dst) in enumerate((
+        (x_in, x_out), (k0, k_out.at[0]), (k1, k_out.at[1]), (v0, v_out.at[0]), (v1, v_out.at[1])))]
+    for copy in copies:
+        copy.start()
+    for copy in copies:
+        copy.wait()
+
+
+def pack(*arrays):
+    cache = jax.ShapeDtypeStruct((2, TOK, HEAD), BF16)
+    return pl.pallas_call(
+        pack_kernel,
+        name='pack',
+        out_shape=(jax.ShapeDtypeStruct((TOK, D), BF16), cache, cache),
+        in_specs=[pl.BlockSpec(memory_space=pltpu.VMEM)] * 5,
+        out_specs=(pl.BlockSpec(memory_space=pl.ANY),) * 3,
+        scratch_shapes=[pltpu.SemaphoreType.DMA((5,))],
+    )(*arrays)
 
 
 def solution(mesh):
@@ -356,14 +378,16 @@
     cache_spec = P(None, ('dp', 'cp'), 'tp', None)
 
     def device_fn(hidden, positions, w_q, w_k, w_v, w_o, w_gate, w_up, w_down, norm_gain, qk_gain):
-        pos = positions.astype(F32)[:, None]
-        exponent = -(jnp.arange(HALF, dtype=F32) * 2.0) / HEAD
-        angles = jnp.stack([pos * (theta ** exponent) for theta in THETAS])
-        rope = jnp.stack([jnp.cos(angles), jnp.sin(angles)], axis=1)
+        pos = (positions[0] + lax.broadcasted_iota(jnp.int32, (TOK, HALF), 0)).astype(F32)
+        exponent = -(np.arange(HALF) * 2.0) / HEAD
+        inv_freq = np.stack([theta ** exponent for theta in THETAS]).astype(np.float32)
+        angles = pos * inv_freq[:, None, :]
+        rope = (jnp.cos(angles), jnp.sin(angles))
         weights = (w_q, w_k, w_v, w_o, w_gate, w_up, w_down)
         x1, k0, v0 = run_layer(0, hidden, rope, weights, norm_gain, qk_gain)
         x2, k1, v1 = run_layer(1, x1, rope, weights, norm_gain, qk_gain)
-        return x2, jnp.stack([k0, k1])[:, :, None, :], jnp.stack([v0, v1])[:, :, None, :]
+        x2, k_cache, v_cache = pack(x2, k0, k1, v0, v1)
+        return x2, k_cache[:, :, None, :], v_cache[:, :, None, :]
 
     return jax.shard_map(
         device_fn,

time: 335 us -> 266 us (0.79)
  Pallas kernels: 326 us -> 261 us
    pallas_call x2, Pallas kernels: 326 us -> 258 us  [run_layer(): pl.pallas_call(functools.partial(layer_kernel, layer), name=f'layer_{laye...]
    unnamed x2 -> x0, other arithmetic: 3.39 us -> none
where the time goes in v2:
time: 266 us
  Pallas kernels  261 us (98%)
  other arithmetic  3.15 us (1%)
    pallas_call x2, Pallas kernels, run_layer(): pl.pallas_call(functools.partial(layer_kernel, layer), name=f'layer_{laye...  258 us

profile of v2, /device:TPU:4, one launch (start us, length us, event | category | flops | bytes accessed | tf_op | source)
XLA Modules:
  0.0 265.8 jit_solution(10415974201858451894)
XLA Ops:
  0.6 1.2 slice.3
  1.8 0.6 add_convert_fusion
  2.5 2.5 multiply_sine_fusion
  5.0 131.9 %layer_0.1 = (bf16[256,2304]{1,0:T(8,128)(2,1)}, bf16[256,256]{1,0:T(8,128)(2,1)}, bf16[256,256]{1,0:T(8,128)(2,1)}) custom-call(bf16[256,2304]{1,0:T(8,128)(2,1)} %x_ref.1, f32[2,256,128]{2,1,0:T(8,128)} %get-tuple-element.25.cos_ref, f32[2,256,128]{2,1,0:T(8,128)} %get-tuple-element.24.sin_ref, bf16[2,2304,512]{2,1,0:T(8,128)(2,1)} %wq_hbm.3, ...), custom_call_target="tpu_custom_call" | custom-call | tf_op jit(solution)/shard_map/layer_0/pallas_call | solution.py:311
  136.9 126.0 %layer_1.1 = (bf16[256,2304]{1,0:T(8,128)(2,1)}, bf16[256,256]{1,0:T(8,128)(2,1)}, bf16[256,256]{1,0:T(8,128)(2,1)}) custom-call(bf16[256,2304]{1,0:T(8,128)(2,1)} %get-tuple-element.12.x_ref, f32[2,256,128]{2,1,0:T(8,128)} %get-tuple-element.25.cos_ref, f32[2,256,128]{2,1,0:T(8,128)} %get-tuple-element.24.sin_ref, bf16[2,2304,512]{2,1,0:T(8,128)(2,1)} %wq_hbm.3, ...), custom_call_target="tpu_custom_call" | custom-call | tf_op jit(solution)/shard_map/layer_1/pallas_call | solution.py:311
  263.0 2.6 pack.1
